TPU v7x, 512 devices: a whole 4x8x8 slice. The times are simulated.
512 devices in a mesh: section: 4 (over x), wide: 32 (over y_hi, z, core), narrow: 4 (over y_lo).
Axes of the slice: x: 4, y: 8 (y_hi: 2, y_lo: 4; y = y_hi * 4 + y_lo), z: 8, core: 2. Of those that a mesh axis runs over, the one named last changes fastest.
Arguments:
- valence_orbitals: float32 [8, 48, 2304], P(None, 'narrow'), may hold values from -6 to 6
- conduction_orbitals: float32 [128, 48, 2304], P(('section', 'wide'), 'narrow'), may hold values from -6 to 6
- valence_energy: float32 [8], replicated, may hold values from -7 to -1
- conduction_energy: float32 [128], replicated, may hold values from 1 to 7
- frequency: float32 [1], replicated, may hold values from 0.5 to 4
- pair_bands: int32 [512, 2], P(('section', 'wide')), may hold values from 0 to 127, as said below
- gvec_index: int32 [12288], replicated, may hold values from 0 to 110591, as said below
Outputs:
- chi: float32 [12288, 12288], P(('section', 'narrow'), 'wide')
Inputs may be any that keep to these rules, and one draw needn't show every extreme that they name: `pair_bands`: column 0 is a valence band, column 1 a conduction band; rows b * 4 to (b + 1) * 4 - 1 pair conduction band b with 4 distinct valence bands. `gvec_index`: the 12288 indices are distinct.
All inputs are finite; a program needn't handle non-finite values.
Results may differ from a plain program's by a relative error of at most 0.000094.
Values sent between devices are 32-bit elements; how exact they have to be, the bound alone decides.
A program may use at most 192 MiB of HBM per device.

v0:
```python
import math

import jax
import jax.numpy as jnp
from jax import lax
from jax.sharding import PartitionSpec as P


def sent_to_all(shard, axis):
    devices = lax.axis_size(axis)
    return lax.all_to_all(
        jnp.broadcast_to(shard[None], (devices, *shard.shape)), axis, 0, 0, tiled=True
    )


def taken_together(shard, axis):
    everything = sent_to_all(shard, axis)
    return jnp.sum(everything, axis=0)


def laid_out(parts, dim):
    parts = jnp.moveaxis(parts, 0, dim)
    dims = parts.shape
    return parts.reshape(*dims[:dim], dims[dim] * dims[dim + 1], *dims[dim + 2 :])


def collect(shard, axis, dim):
    parts = sent_to_all(shard, axis)
    return laid_out(parts, dim)


def build_cosine(length):
    wavenumber = jnp.arange(length, dtype=jnp.float32)[:, None]
    position = jnp.arange(length, dtype=jnp.float32)[None, :]
    cosine = math.sqrt(2.0 / length) * jnp.cos(
        math.pi * (2.0 * position + 1.0) * wavenumber / (2.0 * length)
    )
    return jnp.where(wavenumber == 0.0, cosine * math.sqrt(0.5), cosine)


def contract(left_rows, right_rows):
    return lax.dot_general(
        left_rows,
        right_rows,
        (((0,), (0,)), ((), ())),
        precision=lax.Precision.HIGHEST,
        preferred_element_type=jnp.float32,
    )


def on_device(
    valence_orbitals,
    conduction_orbitals,
    valence_energy,
    conduction_energy,
    frequency,
    pair_bands,
    gvec_index,
):
    highest = lax.Precision.HIGHEST
    planes = valence_orbitals.shape[1]
    narrow_count = lax.axis_size("narrow")
    extent = planes * narrow_count
    pair_count = pair_bands.shape[0]
    section_count = lax.axis_size("section")
    wide_count = lax.axis_size("wide")
    total_pairs = pair_count * section_count * wide_count
    vector_count = gvec_index.shape[0]
    row_block = vector_count // (section_count * narrow_count)
    column_block = vector_count // wide_count
    cosine = build_cosine(extent)
    narrow_pos = lax.axis_index("narrow")
    local_table = lax.dynamic_slice_in_dim(cosine, narrow_pos * planes, planes, 1)
    band_offset = (
        lax.axis_index("section") * wide_count + lax.axis_index("wide")
    ) * conduction_orbitals.shape[0]
    local_band = pair_bands[:, 1] - band_offset
    valence_pick = valence_orbitals[pair_bands[:, 0]].reshape(pair_count, planes, extent, extent)
    conduction_pick = conduction_orbitals[local_band].reshape(pair_count, planes, extent, extent)
    density = valence_pick * conduction_pick
    sweep_one = jnp.einsum("pxyz,kz->pxyk", density, cosine, precision=highest)
    sweep_two = jnp.einsum("pxyk,jy->pxjk", sweep_one, cosine, precision=highest)
    sweep_three = jnp.einsum("pxjk,ix->pijk", sweep_two, local_table, precision=highest)
    partial_value = sweep_three.reshape(pair_count, -1)[:, gvec_index]
    energy_gap = conduction_energy[pair_bands[:, 1]] - valence_energy[pair_bands[:, 0]]
    weight = (
        -4.0
        * energy_gap
        / (energy_gap * energy_gap + frequency[0] * frequency[0])
        / math.sqrt(total_pairs)
    )
    coefficients = taken_together(partial_value, "narrow")
    grouped = coefficients.reshape(pair_count, section_count, narrow_count, row_block)
    own_rows = lax.dynamic_slice_in_dim(grouped, narrow_pos, 1, 2)
    row_send = (own_rows * weight[:, None, None, None]).reshape(
        pair_count, section_count, row_block
    )
    row_recv = lax.all_to_all(row_send, "section", split_axis=1, concat_axis=0, tiled=True).reshape(
        section_count, pair_count, row_block
    )
    column_send = coefficients.reshape(pair_count, wide_count, column_block)
    column_recv = lax.all_to_all(
        column_send, "wide", split_axis=1, concat_axis=0, tiled=True
    ).reshape(wide_count * pair_count, column_block)
    rows_all = collect(row_recv, "wide", 1).reshape(-1, row_block)
    return contract(rows_all, collect(column_recv, "section", 0))


def solution(mesh):
    in_specs = (
        P(None, "narrow", None),
        P(("section", "wide"), "narrow", None),
        P(),
        P(),
        P(),
        P(("section", "wide"), None),
        P(),
    )
    out_specs = P(("section", "narrow"), "wide")
    return jax.shard_map(
        on_device, mesh=mesh, in_specs=in_specs, out_specs=out_specs, check_vma=False
    )
```

profile of v0, /device:TPU:1, one launch (start us, length us, event | category | flops | bytes accessed | tf_op | source)
XLA Modules:
  0.0 234.3 jit_solution(16492378447279550938)
XLA Ops:
  0.0 0.0 copy-start
  0.0 0.8 fusion.9
  0.8 0.8 fusion.3
  1.6 0.9 copy.55
  2.6 0.0 copy-done
  2.6 1.6 gather_fusion
  4.1 0.1 broadcast_multiply_fusion
  4.3 0.8 mul.129
  5.1 0.2 multiply_select_fusion
  5.3 1.2 fusion.1
  6.5 1.3 convolution_bitcast_fusion.1
  7.8 5.6 %convolution_bitcast_fusion = f32[4,48,48,48]{3,1,2,0:T(8,128)} fusion(f32[4,12,48,48]{3,2,1,0:T(8,128)S(1)} %convolution_bitcast_fusion.1, f32[48,48]{0,1:T(8,128)S(1)} %multiply_select_fusion, s32[]{:T(128)S(6)} %select_n.31), kind=kOutput, calls=%fused_computation.4 | convolution fusion | flops 63700992 | bytes 2957316 | tf_op jit(solution)/shard_map/pxjk,ix->pijk/dot_general | solution.py:83
  13.4 27.9 %copy.45 = f32[4,48,48,48]{0,3,2,1:T(8,128)} copy(f32[4,48,48,48]{3,1,2,0:T(8,128)} %convolution_bitcast_fusion) | data formatting | bytes 3538944 | tf_op jit(solution)/shard_map/reshape | solution.py:84
  41.2 58.3 %gather_fusion.1 = f32[12288,4]{1,0:T(8,128)} fusion(f32[4,110592]{0,1:T(8,128)} %bitcast.46, s32[12288]{0:T(1024)S(1)} %fusion.3), kind=kCustom, calls=%fused_computation.1 | custom fusion | bytes 442368 | tf_op jit(solution)/shard_map/gather | solution.py:84
  99.6 4.4 %copy.36 = f32[4,12288]{1,0:T(4,128)S(1)} copy(f32[4,12288]{0,1:T(8,128)} %bitcast.47) | data formatting | bytes 393216 | tf_op jit(solution)/shard_map/gather | solution.py:84
  104.0 0.0 copy-start.2
  104.0 0.0 copy-start.3
  104.0 1.0 broadcast_in_dim.44
  105.0 5.4 %all-to-all-start = ((f32[4,4,12288]{2,1,0:T(4,128)}), f32[4,4,12288]{2,1,0:T(4,128)S(1)}, u32[]{:S(2)}, u32[]{:S(2)}) async-start(f32[4,4,12288]{2,1,0:T(4,128)} %broadcast_in_dim.44), calls=%async_computation | async-start | bytes 1572864 | tf_op jit(solution)/shard_map/all_to_all | solution.py:11
  111.1 0.0 copy-done.2
  111.1 0.6 gather_fusion.3
  111.7 0.0 copy-done.3
  111.7 0.6 gather_fusion.2
  112.4 13.2 %all-to-all-done = f32[4,4,12288]{2,1,0:T(4,128)S(1)} async-done(((f32[4,4,12288]{2,1,0:T(4,128)}), f32[4,4,12288]{2,1,0:T(4,128)S(1)}, u32[]{:S(2)}, u32[]{:S(2)}) %all-to-all-start) | async-done | bytes 786464 | tf_op jit(solution)/shard_map/all_to_all | solution.py:11
  125.5 0.2 reduce_sum.9
  125.8 0.2 reshape.51
  125.9 0.1 dynamic-slice_multiply_fusion
  126.1 12.7 %all_to_all.45 = f32[4,4,768]{2,0,1:T(4,128)S(1)} all-to-all(f32[4,4,768]{2,0,1:T(4,128)S(1)} %bitcast.54), channel_id=1, replica_groups=mesh['section'=4,'wide'=32,'narrow'=4] {'section'}, dimensions={1} | all-to-all | bytes 98304 | tf_op jit(solution)/shard_map/all_to_all | solution.py:98
  138.8 29.7 %all_to_all.46 = f32[4,32,384]{2,0,1:T(4,128)S(1)} all-to-all(f32[4,32,384]{2,0,1:T(4,128)S(1)} %bitcast.50), channel_id=1, replica_groups=mesh['section'=4,'wide'=32,'narrow'=4] {'wide'}, dimensions={1} | all-to-all | bytes 393216 | tf_op jit(solution)/shard_map/all_to_all | solution.py:102
  168.5 1.5 broadcast_in_dim.46
  170.0 5.5 %all-to-all-start.2 = ((f32[32,4,4,768]{3,2,1,0:T(4,128)}), f32[32,4,4,768]{3,2,1,0:T(4,128)S(1)}, u32[]{:S(2)}, u32[]{:S(2)}) async-start(f32[32,4,4,768]{3,2,1,0:T(4,128)} %broadcast_in_dim.46), calls=%async_computation.2 | async-start | bytes 3145728 | tf_op jit(solution)/shard_map/all_to_all | solution.py:11
  175.5 0.1 broadcast_in_dim.47
  175.6 40.8 %all-to-all-done.2 = f32[32,4,4,768]{3,2,1,0:T(4,128)S(1)} async-done(((f32[32,4,4,768]{3,2,1,0:T(4,128)}), f32[32,4,4,768]{3,2,1,0:T(4,128)S(1)}, u32[]{:S(2)}, u32[]{:S(2)}) %all-to-all-start.2) | async-done | bytes 1572896 | tf_op jit(solution)/shard_map/all_to_all | solution.py:11
  216.4 0.9 broadcast_in_dim.48
  217.3 3.7 %all-to-all-start.4 = ((f32[4,128,384]{2,1,0:T(8,128)}), f32[4,128,384]{2,1,0:T(8,128)S(1)}, u32[]{:S(2)}, u32[]{:S(2)}) async-start(f32[4,128,384]{2,1,0:T(8,128)} %broadcast_in_dim.48), calls=%async_computation.4 | async-start | bytes 1572864 | tf_op jit(solution)/shard_map/all_to_all | solution.py:11
  221.0 1.2 copy.38
  222.3 1.8 reshape_reshape.3
  224.1 6.5 %all-to-all-done.4 = f32[4,128,384]{2,1,0:T(8,128)S(1)} async-done(((f32[4,128,384]{2,1,0:T(8,128)}), f32[4,128,384]{2,1,0:T(8,128)S(1)}, u32[]{:S(2)}, u32[]{:S(2)}) %all-to-all-start.4) | async-done | bytes 786464 | tf_op jit(solution)/shard_map/all_to_all | solution.py:11
  230.6 0.0 copy-start.1
  230.6 3.7 %fusion.18 = f32[768,384]{1,0:T(8,128)} fusion(f32[512,768]{1,0:T(8,128)S(1)} %reshape_reshape.3, f32[512,384]{1,0:T(8,128)S(1)} %bitcast.49), kind=kOutput, calls=%fused_computation.37 | convolution fusion | flops 1811939328 | bytes 3538944 | tf_op jit(solution)/shard_map/dot_general | solution.py:42
  234.3 0.0 copy-done.1
  (5 shorter events, 0.1 us)
Async XLA Ops:
  0.0 2.6 %copy-start = (f32[8,12,2304]{2,0,1:T(8,128)S(1)}, f32[8,12,2304]{2,0,1:T(8,128)}, u32[]{:S(2)}) copy-start(f32[8,12,2304]{2,0,1:T(8,128)} %param.7) | copy-start | bytes 2654212
  104.0 7.1 %copy-start.2 = (f32[8]{0:T(128)S(1)}, f32[8]{0:T(128)}, u32[]{:S(2)}) copy-start(f32[8]{0:T(128)} %param.9) | copy-start | bytes 100
  104.0 7.7 %copy-start.3 = (f32[128]{0:T(128)S(1)}, f32[128]{0:T(128)}, u32[]{:S(2)}) copy-start(f32[128]{0:T(128)} %param.10) | copy-start | bytes 1540
  105.0 20.5 %all-to-all-start = ((f32[4,4,12288]{2,1,0:T(4,128)}), f32[4,4,12288]{2,1,0:T(4,128)S(1)}, u32[]{:S(2)}, u32[]{:S(2)}) async-start(f32[4,4,12288]{2,1,0:T(4,128)} %broadcast_in_dim.44), calls=%async_computation | async-start | bytes 1572864 | tf_op jit(solution)/shard_map/all_to_all | solution.py:11
  170.0 46.4 %all-to-all-start.2 = ((f32[32,4,4,768]{3,2,1,0:T(4,128)}), f32[32,4,4,768]{3,2,1,0:T(4,128)S(1)}, u32[]{:S(2)}, u32[]{:S(2)}) async-start(f32[32,4,4,768]{3,2,1,0:T(4,128)} %broadcast_in_dim.46), calls=%async_computation.2 | async-start | bytes 3145728 | tf_op jit(solution)/shard_map/all_to_all | solution.py:11
  217.3 13.3 %all-to-all-start.4 = ((f32[4,128,384]{2,1,0:T(8,128)}), f32[4,128,384]{2,1,0:T(8,128)S(1)}, u32[]{:S(2)}, u32[]{:S(2)}) async-start(f32[4,128,384]{2,1,0:T(8,128)} %broadcast_in_dim.48), calls=%async_computation.4 | async-start | bytes 1572864 | tf_op jit(solution)/shard_map/all_to_all | solution.py:11
  230.6 3.7 %copy-start.1 = (f32[8,12,2304]{2,0,1:T(8,128)S(1)}, f32[8,12,2304]{2,0,1:T(8,128)}, u32[]{:S(2)}) copy-start(f32[8,12,2304]{2,0,1:T(8,128)} %param.7) | copy-start | bytes 2654212
where the time goes:
time: 237 us; the launch traced here: 234 us
  local copies, waits for them, and re-layouts  102 us (43%)
  waiting for transfers between devices  60.5 us (26%)
  blocking collectives  42.5 us (18%)
  starting transfers between devices  14.6 us (6%)
  matrix products  11.8 us (5%)
    gather x2, local copies, waits for them, and re-layouts, on_device(): partial_value = sweep_three.reshape(pair_count, -1)[:, gvec_index]  62.8 us
    all_to_all x3, waiting for transfers between devices, sent_to_all(): lax.all_to_all(jnp.broadcast_to(shard[None], (devices, *shard.shape)), ax...  60.5 us
    all_to_all x1, blocking collectives, on_device(): lax.all_to_all(column_send, 'wide', split_axis=1, concat_axis=0, tiled=True)  29.7 us
    reshape x1, local copies, waits for them, and re-layouts, on_device(): partial_value = sweep_three.reshape(pair_count, -1)[:, gvec_index]  27.9 us
    all_to_all x3, starting transfers between devices, sent_to_all(): lax.all_to_all(jnp.broadcast_to(shard[None], (devices, *shard.shape)), ax...  14.6 us
    all_to_all x1, blocking collectives, on_device(): lax.all_to_all(row_send, 'section', split_axis=1, concat_axis=0, tiled=True)  12.7 us
    dot_general x1, matrix products, on_device(): jnp.einsum('pxjk,ix->pijk', sweep_two, local_table, precision=highest)  5.58 us
  transfers between devices with their start and end apart: 3, of which 3 were waited for; matrix products, arithmetic and copies ran while one was open for 2% of the time, Pallas kernels for 0%

commit v1 on v0

v1 whole, which is shorter than its diff:
```python
import functools
import math

import jax
import jax.numpy as jnp
import numpy as np
from jax import lax
from jax.experimental import pallas as pl
from jax.experimental.pallas import tpu as pltpu
from jax.sharding import PartitionSpec as P

F32, BF16 = jnp.float32, jnp.bfloat16
MESH = pl.DeviceIdType.MESH
GRID, NARROW, SECTION = 48, 4, 4
HIGH, RING, CORES = 2, 8, 2
WIDE = HIGH * RING * CORES
PLANES = GRID // NARROW
AREA = GRID * GRID
VECTORS = 12288
ROWS, COLS = VECTORS // 16, VECTORS // 32


def split_np(a):
    a = np.asarray(a, np.float32)
    h = a.astype(BF16)
    return h, (a - h.astype(np.float32)).astype(BF16)


def tables():
    k, x = np.arange(GRID)[:, None], np.arange(GRID)[None, :]
    c = math.sqrt(2.0 / GRID) * np.cos(math.pi * (2 * x + 1) * k / (2 * GRID))
    c[0] *= math.sqrt(0.5)
    cx = np.zeros((64, GRID))
    order = [p * PLANES + q for p in range(4) for q in range(8)] + [p * PLANES + q for p in range(4) for q in range(8, 12)]
    for i in range(GRID):
        cx[(i // 6) * 8 + i % 6] = c[i, order]
    h, l = split_np(cx)
    cx3 = np.concatenate([h, l, h], axis=1)
    bh, bl = split_np(np.kron(np.eye(16), c.T))
    h, l = split_np(c)
    cy3 = np.concatenate([h, l, h], axis=1)
    return cx3, bh, bl, cy3


def hi_lo(a):
    h = a.astype(BF16)
    return h, (a - h.astype(F32)).astype(BF16)


def dot(a, b):
    return lax.dot_general(a, b, (((1,), (0,)), ((), ())), preferred_element_type=F32)


def exchange_body(
    bands_ref, valence_ref, conduction_ref, out8_ref, out4_ref, stage8_ref, stage4_ref, send_sem, recv_sem
):
    me = lax.axis_index("narrow")
    barrier = pltpu.get_barrier_semaphore()
    for d in range(1, NARROW):
        pl.semaphore_signal(
            barrier, inc=1, device_id={"narrow": lax.rem(me + d, NARROW)}, device_id_type=MESH
        )
    conduction = conduction_ref[0]
    for p in range(NARROW):
        density = valence_ref[bands_ref[p, 0]] * conduction
        stage8_ref[p] = density[:8]
        stage4_ref[p] = density[8:]
    out8_ref[me] = stage8_ref[me]
    out4_ref[me] = stage4_ref[me]
    pl.semaphore_wait(barrier, NARROW - 1)
    copies = []
    for d in range(1, NARROW):
        peer = lax.rem(me + d, NARROW)
        for part, (src, dst) in enumerate(((stage8_ref, out8_ref), (stage4_ref, out4_ref))):
            copy = pltpu.make_async_remote_copy(
                src_ref=src.at[peer],
                dst_ref=dst.at[me],
                send_sem=send_sem.at[part, d - 1],
                recv_sem=recv_sem.at[part, d - 1],
                device_id={"narrow": peer},
                device_id_type=MESH,
            )
            copy.start()
            copies.append(copy)
    for copy in copies:
        copy.wait()


def exchange(bands, valence, conduction):
    return pl.pallas_call(
        exchange_body,
        out_shape=(
            jax.ShapeDtypeStruct((NARROW, 8, AREA), F32),
            jax.ShapeDtypeStruct((NARROW, 4, AREA), F32),
        ),
        in_specs=[
            pl.BlockSpec(memory_space=pltpu.SMEM),
            pl.BlockSpec(memory_space=pltpu.VMEM),
            pl.BlockSpec(memory_space=pltpu.VMEM),
        ],
        out_specs=(pl.BlockSpec(memory_space=pltpu.VMEM), pl.BlockSpec(memory_space=pltpu.VMEM)),
        scratch_shapes=[
            pltpu.VMEM((NARROW, 8, AREA), F32),
            pltpu.VMEM((NARROW, 4, AREA), F32),
            pltpu.SemaphoreType.DMA((2, NARROW - 1)),
            pltpu.SemaphoreType.DMA((2, NARROW - 1)),
        ],
        compiler_params=pltpu.CompilerParams(collective_id=0, has_side_effects=True),
        name="exchange",
    )(bands, valence, conduction)


def coefficients_body(
    bands_ref, ve_ref, ce_ref, freq_ref, d8_ref, d4_ref, rid_ref, lid_ref, cx_ref, bh_ref, bl_ref, cy_ref,
    row_ref, col_ref, z_ref, s_ref, t_ref, tt_ref,
):
    me = lax.axis_index("narrow")
    valence = jnp.full((1, ROWS), ve_ref[bands_ref[me, 0]], F32)
    conduction = jnp.full((1, ROWS), ce_ref[bands_ref[me, 1]], F32)
    frequency = jnp.full((1, ROWS), freq_ref[0], F32)
    gap = conduction - valence
    weight = -4.0 * gap / (gap * gap + frequency * frequency) / math.sqrt(512.0)

    last = [jnp.concatenate([d4_ref[2 * q], d4_ref[2 * q + 1]], axis=0) for q in range(2)]
    dh, dl = hi_lo(jnp.concatenate([d8_ref[...].reshape(32, AREA), *last], axis=0))
    a = dot(cx_ref[...], jnp.concatenate([dh, dh, dl], axis=0))
    ah, al = hi_lo(a)
    third = AREA // 3
    lhs = jnp.concatenate(
        [half[:, b * third : (b + 1) * third] for half in (ah, al) for b in range(3)], axis=0
    )
    by_high = dot(lhs, bh_ref[...])
    by_low = dot(lhs[:192], bl_ref[...])
    for b in range(3):
        rows = slice(b * 64, (b + 1) * 64)
        z_ref[:, b * third : (b + 1) * third] = (
            by_high[rows] + by_high[192 + b * 64 : 256 + b * 64] + by_low[rows]
        )

    def relay(group, carry):
        part = z_ref[:, pl.ds(pl.multiple_of(group * 384, 128), 384)]
        for y in range(8):
            s_ref[group * 8 + y] = jnp.concatenate(
                [part[i * 8 : (i + 1) * 8, y * GRID : (y + 1) * GRID] for i in range(8)], axis=1
            )
        return carry

    lax.fori_loop(0, 6, relay, 0)
    for r in range(6):
        sh, sl = hi_lo(s_ref[:, r, :])
        t = dot(cy_ref[...], jnp.concatenate([sh, sh, sl], axis=0))
        for u in range(3):
            t_ref[(r * 3 + u) * GRID : (r * 3 + u + 1) * GRID, :] = t[:, u * 128 : (u + 1) * 128]
    th, tl = hi_lo(t_ref[...].T)
    tt_ref[0:128, :864] = th
    tt_ref[128:256, :864] = tl

    def chunk(k, carry):
        parts = []
        for q in range(3):
            here = pl.ds(pl.multiple_of(k * ROWS + q * 256, 256), 256)
            rid, lid = rid_ref[0:1, here], lid_ref[0:1, here]
            acc = None
            for kt in range(4):
                kn = min(256, 864 - kt * 256)
                index = lax.broadcasted_iota(jnp.int32, (kn, 256), 0) + kt * 256
                hot = jnp.where(index == rid, 1.0, 0.0).astype(BF16)
                part = dot(tt_ref[:, kt * 256 : kt * 256 + kn], hot)
                acc = part if acc is None else acc + part
            both = acc[:128] + acc[128:]
            mine = lax.broadcasted_iota(jnp.int32, (128, 256), 0) == lid
            parts.append(jnp.sum(jnp.where(mine, both, 0.0), axis=0, keepdims=True))
        c = jnp.concatenate(parts, axis=1)
        row_ref[k] = c * weight
        col_ref[2 * k] = c[:, :COLS]
        col_ref[2 * k + 1] = c[:, COLS:]
        return carry

    lax.fori_loop(0, 16, chunk, 0)


def coefficients(bands, ve, ce, freq, d8, d4, rid, lid):
    smem, vmem = pl.BlockSpec(memory_space=pltpu.SMEM), pl.BlockSpec(memory_space=pltpu.VMEM)
    return pl.pallas_call(
        coefficients_body,
        out_shape=(
            jax.ShapeDtypeStruct((16, 1, ROWS), F32),
            jax.ShapeDtypeStruct((32, 1, COLS), F32),
        ),
        in_specs=[smem] * 4 + [vmem] * 8,
        out_specs=(vmem, vmem),
        scratch_shapes=[
            pltpu.VMEM((64, AREA), F32),
            pltpu.VMEM((GRID, 8, 384), F32),
            pltpu.VMEM((864, 128), F32),
            pltpu.VMEM((256, 896), BF16),
        ],
        compiler_params=pltpu.CompilerParams(vmem_limit_bytes=40 * 1024 * 1024),
        name="coefficients",
    )(bands, ve, ce, freq, d8, d4, rid, lid, *[jnp.asarray(t) for t in tables()])


def gather_body(row_ref, col_ref, rows_ref, cols_ref, cbuf_ref, send_small, send_row, send_side, send_col,
                recv_row1, recv_col1, recv_ring, recv_side, recv_y, recv_x, recv_xx):
    s, w, n = lax.axis_index("section"), lax.axis_index("wide"), lax.axis_index("narrow")
    yh, z, c = w // 16, lax.rem(w // 2, RING), lax.rem(w, 2)
    barrier = pltpu.get_barrier_semaphore()

    def row_peer(d):
        sp, np_ = lax.rem(s + lax.rem(d, 4), 4), lax.rem(n + lax.rem(d // 4, 4), 4)
        wp = lax.rem(yh + d // 16, 2) * 16 + z * 2 + c
        return sp, wp, np_

    def col_peer(d):
        return lax.rem(w + d, WIDE)

    def greet(d, carry):
        sp, wp, np_ = row_peer(d)
        pl.semaphore_signal(barrier, inc=1, device_id={"section": sp, "wide": wp, "narrow": np_}, device_id_type=MESH)
        pl.semaphore_signal(barrier, inc=1, device_id={"wide": col_peer(d)}, device_id_type=MESH)
        return carry

    lax.fori_loop(1, 32, greet, 0)
    block = (z * 2 + c) * 32
    home = block + yh * 16 + s * 4 + n
    from_me = (z * 2 + c) * 2 + yh
    rows_ref[home] = row_ref[s * 4 + n]
    cbuf_ref[from_me] = col_ref[w]
    pl.semaphore_wait(barrier, 62)

    def spread(d, carry):
        sp, wp, np_ = row_peer(d)
        pltpu.make_async_remote_copy(
            src_ref=row_ref.at[sp * 4 + np_], dst_ref=rows_ref.at[home], send_sem=send_small,
            recv_sem=recv_row1.at[d // 16],
            device_id={"section": sp, "wide": wp, "narrow": np_}, device_id_type=MESH,
        ).start()
        wc = col_peer(d)
        pltpu.make_async_remote_copy(
            src_ref=col_ref.at[wc], dst_ref=cbuf_ref.at[from_me], send_sem=send_small,
            recv_sem=recv_col1, device_id={"wide": wc}, device_id_type=MESH,
        ).start()
        return carry

    lax.fori_loop(1, 32, spread, 0)

    def sub(zz, cc, h):
        return rows_ref.at[pl.ds((zz * 2 + cc) * 32 + lax.rem(yh + h, 2) * 16, 16)]

    def ring_peer(step):
        return yh * 16 + lax.rem(z + step + RING, RING) * 2 + c

    side = yh * 16 + z * 2 + (1 - c)
    sends = []

    def send(ref, send_sem, recv_sem, **device):
        copy = pltpu.make_async_remote_copy(
            src_ref=ref, dst_ref=ref, send_sem=send_sem, recv_sem=recv_sem, device_id=device, device_id_type=MESH
        )
        copy.start()
        sends.append(copy)

    def arrived(ref, sem):
        pltpu.make_async_copy(ref, ref, sem).wait()

    arrived(cbuf_ref.at[pl.ds(0, 31)], recv_col1)
    own_cols = cols_ref.at[s * 4 + n]
    cols_ref[s * 4 + n] = cbuf_ref[...]
    for d in range(1, NARROW):
        copy = pltpu.make_async_remote_copy(
            src_ref=cbuf_ref, dst_ref=own_cols, send_sem=send_col, recv_sem=recv_y.at[d - 1],
            device_id={"narrow": lax.rem(n + d, NARROW)}, device_id_type=MESH,
        )
        copy.start()
        sends.append(copy)
    for i, step in enumerate((1, -1)):
        copy = pltpu.make_async_remote_copy(
            src_ref=cbuf_ref, dst_ref=own_cols, send_sem=send_col, recv_sem=recv_x.at[0, i],
            device_id={"section": lax.rem(s + step + SECTION, SECTION)}, device_id_type=MESH,
        )
        copy.start()
        sends.append(copy)

    for h in range(2):
        arrived(rows_ref.at[pl.ds(0, 15 + h)], recv_row1.at[h])
        send(sub(z, c, h), send_row, recv_ring.at[0, 0, h], wide=ring_peer(1))
        send(sub(z, c, h), send_row, recv_ring.at[1, 0, h], wide=ring_peer(-1))
        send(sub(z, c, h), send_side, recv_side.at[0, 0, h], wide=side)

    def cols_of(ds, d):
        return cols_ref.at[lax.rem(s + ds + SECTION, SECTION) * 4 + lax.rem(n - d + NARROW, NARROW)]

    for k in range(1, 5):
        if k < NARROW:
            got = cols_of(0, k)
            arrived(got, recv_y.at[k - 1])
            send(got, send_col, recv_x.at[k, 0], section=lax.rem(s + 1, SECTION))
            send(got, send_col, recv_x.at[k, 1], section=lax.rem(s + SECTION - 1, SECTION))
        for h in range(2):
            for i, step in ((0, 1), (1, -1)):
                if k == 4 and h != i:
                    continue
                got = sub(lax.rem(z - step * k + RING, RING), c, h)
                arrived(got, recv_ring.at[i, k - 1, h])
                if k < 3 or (k == 3 and h == i):
                    send(got, send_row, recv_ring.at[i, k, h], wide=ring_peer(step))
                send(got, send_side, recv_side.at[i, k, h], wide=side)
    for d in range(NARROW):
        i, step = (0, 1) if d % 2 == 0 else (1, -1)
        got = cols_of(-step, d)
        arrived(got, recv_x.at[d, i])
        send(got, send_col, recv_xx.at[d], section=lax.rem(s + step + SECTION, SECTION))
    for d in range(NARROW):
        i, step = (1, -1) if d % 2 == 0 else (0, 1)
        arrived(cols_of(-step, d), recv_x.at[d, i])
        arrived(cols_of(2, d), recv_xx.at[d])
    for h in range(2):
        arrived(sub(z, 1 - c, h), recv_side.at[0, 0, h])
        for k in range(1, 5):
            for i, step in ((0, 1), (1, -1)):
                if k == 4 and h != i:
                    continue
                arrived(sub(lax.rem(z - step * k + RING, RING), 1 - c, h), recv_side.at[i, k, h])
    for copy in sends:
        copy.wait_send()
    arrived(rows_ref.at[pl.ds(0, 31)], send_small)
    arrived(cbuf_ref.at[pl.ds(0, 31)], send_small)


def gather(row, col):
    vmem = pl.BlockSpec(memory_space=pltpu.VMEM)
    dma = pltpu.SemaphoreType.DMA
    return pl.pallas_call(
        gather_body,
        out_shape=(
            jax.ShapeDtypeStruct((512, 1, ROWS), F32),
            jax.ShapeDtypeStruct((16, WIDE, 1, COLS), F32),
        ),
        in_specs=[vmem, vmem],
        out_specs=(vmem, vmem),
        scratch_shapes=[
            pltpu.VMEM((WIDE, 1, COLS), F32),
            dma, dma, dma, dma,
            dma((2,)), dma, dma((2, 4, 2)), dma((2, 5, 2)), dma((3,)), dma((4, 2)), dma((4,)),
        ],
        compiler_params=pltpu.CompilerParams(collective_id=1, has_side_effects=True),
        name="gather",
    )(row, col)


def product_body(rows_ref, cols_ref, out_ref):
    right = jnp.concatenate([cols_ref[pl.ds(u, 512, stride=3), :] for u in range(3)], axis=1)
    bh, bl = hi_lo(right)
    for t in range(6):
        left = jnp.concatenate(
            [rows_ref[pl.ds(sn * 6 + t, 32, stride=96), :] for sn in range(16)], axis=0
        )
        ah, al = hi_lo(left.T)
        out_ref[t * 128 : (t + 1) * 128, :] = dot(
            jnp.concatenate([ah, ah, al], axis=1), jnp.concatenate([bh, bl, bh], axis=0)
        )


def product(rows, cols):
    return pl.pallas_call(
        product_body,
        out_shape=jax.ShapeDtypeStruct((ROWS, COLS), F32),
        compiler_params=pltpu.CompilerParams(vmem_limit_bytes=40 * 1024 * 1024),
        name="product",
    )(rows.reshape(512 * 6, 128), cols.reshape(512 * 3, 128))


def on_device(ve_orb, ce_orb, ve, ce, freq, bands, gvec):
    i, j, k = gvec // AREA, lax.rem(gvec // GRID, GRID), lax.rem(gvec, GRID)
    lane = (i // 6) * GRID + k
    rid = ((lax.rem(i, 6) * 3 + lane // 128) * GRID + j).reshape(1, -1)
    lid = lax.rem(lane, 128).reshape(1, -1)
    d8, d4 = exchange(bands, ve_orb, ce_orb)
    row, col = coefficients(bands, ve, ce, freq, d8, d4, rid, lid)
    rows, cols = gather(row, col)
    return product(rows, cols)


def solution(mesh):
    in_specs = (
        P(None, "narrow", None),
        P(("section", "wide"), "narrow", None),
        P(),
        P(),
        P(),
        P(("section", "wide"), None),
        P(),
    )
    return jax.shard_map(
        on_device,
        mesh=mesh,
        in_specs=in_specs,
        out_specs=P(("section", "narrow"), "wide"),
        check_vma=False,
    )
```

time: 237 us -> 92.6 us (0.39)
  the two profiles are of different devices: /device:TPU:1 before, /device:TPU:48 now
where the time goes in v1:
time: 92.6 us; the launch traced here: 92.1 us
  Pallas kernels  79.2 us (86%)
  local copies, waits for them, and re-layouts  11.1 us (12%)
  other arithmetic  0.96 us (1%)
    pallas_call x1, Pallas kernels, gather(): pl.pallas_call(gather_body, out_shape=(jax.ShapeDtypeStruct((512, 1, ROWS...  47.9 us
    pallas_call x1, Pallas kernels, exchange(): pl.pallas_call(exchange_body, out_shape=(jax.ShapeDtypeStruct((NARROW, 8,...  14.6 us
    pallas_call x1, Pallas kernels, coefficients(): pl.pallas_call(coefficients_body, out_shape=(jax.ShapeDtypeStruct((16, 1,...  13.7 us
    unnamed x29, local copies, waits for them, and re-layouts  11.1 us
    pallas_call x1, Pallas kernels, product(): pl.pallas_call(product_body, out_shape=jax.ShapeDtypeStruct((ROWS, COLS),...  3.01 us

profile of v1, /device:TPU:48, one launch (start us, length us, event | category | flops | bytes accessed | tf_op | source)
XLA Modules:
  0.0 92.1 jit_solution(3818678782904751576)
XLA Ops:
  0.7 1.3 %copy.15.bands_ref = s32[4,2]{1,0:T(4,128)} copy(s32[4,2]{0,1:T(2,128)} %param.16) | data formatting | bytes 64 | tf_op args[5]
  2.0 1.0 %negate_select_fusion.1 = (s32[12288]{0:T(1024)S(1)}, s32[12288]{0:T(1024)S(1)}) fusion(s32[12288]{0:T(1024)} %param.17), kind=kLoop, calls=%fused_computation.3 | loop fusion | flops 540672 | bytes 147456 | tf_op jit(solution)/shard_map/jit(floor_divide)/rem | solution.py:376
  2.9 1.6 %copy.14.conduction_ref = f32[1,12,2304]{2,1,0:T(8,128)} copy(f32[1,12,2304]{2,0,1:T(1,128)} %param.12) | data formatting | bytes 221184 | tf_op args[1]
  4.5 0.0 copy-start.2
  4.5 2.6 %copy.13.valence_ref = f32[8,12,2304]{2,1,0:T(8,128)} copy(f32[8,12,2304]{2,0,1:T(8,128)} %param.11) | data formatting | bytes 1769472 | tf_op args[0]
  7.1 0.0 copy-start.1
  7.1 0.0 copy-start.8
  7.1 0.0 copy-start.9
  7.1 0.0 copy-start.10
  7.1 0.0 copy-start.11
  7.1 0.0 copy-start.12
  7.1 14.6 %exchange.1 = (f32[4,8,2304]{2,1,0:T(8,128)}, f32[4,4,2304]{2,1,0:T(4,128)}) custom-call(s32[4,2]{1,0:T(4,128)} %copy.15.bands_ref, f32[8,12,2304]{2,1,0:T(8,128)} %copy.13.valence_ref, f32[1,12,2304]{2,1,0:T(8,128)} %copy.14.conduction_ref), custom_call_target="tpu_custom_call" | custom-call | tf_op jit(solution)/shard_map/exchange/pallas_call | solution.py:90
  21.7 0.0 copy-done.2
  21.7 0.0 copy-done.1
  21.8 0.0 copy-done.8
  21.8 0.0 copy-done.9
  21.8 0.0 copy-done.10
  21.8 0.0 copy-done.11
  21.8 0.0 copy-done.12
  21.8 0.0 copy-start.4
  21.8 1.0 %copy-done.4 = f32[4,8,2304]{2,1,0:T(8,128)S(1)} copy-done((f32[4,8,2304]{2,1,0:T(8,128)S(1)}, f32[4,8,2304]{2,1,0:T(8,128)}, u32[]{:S(2)}) %copy-start.4) | copy-done | bytes 294936
  22.8 0.0 copy-start.5
  22.8 0.9 copy-done.5
  23.7 13.7 %coefficients.1 = (f32[16,1,768]{2,1,0:T(1,128)S(1)}, f32[32,1,384]{2,1,0:T(1,128)S(1)}) custom-call(s32[4,2]{1,0:T(4,128)S(1)} %copy-done.10, f32[8]{0:T(128)S(1)} %copy-done.11, f32[128]{0:T(128)S(1)} %copy-done.12, f32[1]{0:T(128)S(6)} %copy.16.freq_ref, f32[4,8,2304]{2,1,0:T(8,128)S(1)} %copy-done.4, f32[4,4,2304]{2,1,0:T(4,128)S(1)} %copy-done.5, ...), custom_call_target="tpu_custom_call" | custom-call | tf_op jit(solution)/shard_map/coefficients/pallas_call | solution.py:184
  37.4 0.0 copy-start.6
  37.4 0.6 copy-done.6
  38.0 0.0 copy-start.7
  38.0 0.6 copy-done.7
  38.6 47.9 %gather.1 = (f32[512,1,768]{2,1,0:T(1,128)}, f32[16,32,1,384]{3,2,1,0:T(1,128)}) custom-call(f32[16,1,768]{2,1,0:T(1,128)} %copy-done.6, f32[32,1,384]{2,1,0:T(1,128)} %copy-done.7), custom_call_target="tpu_custom_call" | custom-call | tf_op jit(solution)/shard_map/gather/pallas_call | solution.py:333
  86.5 0.0 copy-start
  86.5 1.4 %copy-done = f32[512,1,768]{2,1,0:T(1,128)S(1)} copy-done((f32[512,1,768]{2,1,0:T(1,128)S(1)}, f32[512,1,768]{2,1,0:T(1,128)}, u32[]{:S(2)}) %copy-start) | copy-done | bytes 1572888
  87.9 0.0 copy-start.3
  87.9 1.1 %copy-done.3 = f32[16,32,1,384]{3,2,1,0:T(1,128)S(1)} copy-done((f32[16,32,1,384]{3,2,1,0:T(1,128)S(1)}, f32[16,32,1,384]{3,2,1,0:T(1,128)}, u32[]{:S(2)}) %copy-start.3) | copy-done | bytes 786456
  89.1 3.0 %product.1 = f32[768,384]{1,0:T(8,128)} custom-call(f32[3072,128]{1,0:T(8,128)S(1)} %bitcast.4, f32[1536,128]{1,0:T(8,128)S(1)} %bitcast.5), custom_call_target="tpu_custom_call" | custom-call | tf_op jit(solution)/shard_map/product/pallas_call | solution.py:365
Async XLA Ops:
  4.5 17.2 %copy-start.2 = (bf16[768,768]{1,0:T(8,128)(2,1)S(1)}, bf16[768,768]{1,0:T(8,128)(2,1)}, u32[]{:S(2)}) copy-start(bf16[768,768]{1,0:T(8,128)(2,1)} %constant.48.clone.bh_ref) | copy-start | bytes 3538948
  7.1 14.7 %copy-start.1 = (bf16[768,768]{1,0:T(8,128)(2,1)S(1)}, bf16[768,768]{1,0:T(8,128)(2,1)}, u32[]{:S(2)}) copy-start(bf16[768,768]{1,0:T(8,128)(2,1)} %constant.49.clone.bl_ref) | copy-start | bytes 3538948
  7.1 14.7 %copy-start.8 = (bf16[64,144]{1,0:T(8,128)(2,1)S(1)}, bf16[64,144]{1,0:T(8,128)(2,1)}, u32[]{:S(2)}) copy-start(bf16[64,144]{1,0:T(8,128)(2,1)} %constant.47.clone.cx_ref) | copy-start | bytes 55300
  7.1 14.7 %copy-start.9 = (bf16[48,144]{1,0:T(8,128)(2,1)S(1)}, bf16[48,144]{1,0:T(8,128)(2,1)}, u32[]{:S(2)}) copy-start(bf16[48,144]{1,0:T(8,128)(2,1)} %constant.50.clone.cy_ref) | copy-start | bytes 41476
  7.1 14.7 %copy-start.10 = (s32[4,2]{1,0:T(4,128)S(1)}, s32[4,2]{1,0:T(4,128)}, u32[]{:S(2)}) copy-start(s32[4,2]{1,0:T(4,128)} %copy.15.bands_ref) | copy-start | bytes 100
  7.1 14.7 %copy-start.11 = (f32[8]{0:T(128)S(1)}, f32[8]{0:T(128)}, u32[]{:S(2)}) copy-start(f32[8]{0:T(128)} %ve_ref.1) | copy-start | bytes 100
  7.1 14.7 %copy-start.12 = (f32[128]{0:T(128)S(1)}, f32[128]{0:T(128)}, u32[]{:S(2)}) copy-start(f32[128]{0:T(128)} %ce_ref.1) | copy-start | bytes 1540
  21.8 1.0 %copy-start.4 = (f32[4,8,2304]{2,1,0:T(8,128)S(1)}, f32[4,8,2304]{2,1,0:T(8,128)}, u32[]{:S(2)}) copy-start(f32[4,8,2304]{2,1,0:T(8,128)} %get-tuple-element.11.d8_ref) | copy-start | bytes 884740
  22.8 0.9 copy-start.5
  37.4 0.6 copy-start.6
  38.0 0.6 copy-start.7
  86.5 1.4 %copy-start = (f32[512,1,768]{2,1,0:T(1,128)S(1)}, f32[512,1,768]{2,1,0:T(1,128)}, u32[]{:S(2)}) copy-start(f32[512,1,768]{2,1,0:T(1,128)} %get-tuple-element.15) | copy-start | bytes 4718596
  87.9 1.1 %copy-start.3 = (f32[16,32,1,384]{3,2,1,0:T(1,128)S(1)}, f32[16,32,1,384]{3,2,1,0:T(1,128)}, u32[]{:S(2)}) copy-start(f32[16,32,1,384]{3,2,1,0:T(1,128)} %get-tuple-element.16) | copy-start | bytes 2359300

commit v2 on v1

v2 whole, which is shorter than its diff:
```python
import functools
import math

import jax
import jax.numpy as jnp
import numpy as np
from jax import lax
from jax.experimental import pallas as pl
from jax.experimental.pallas import tpu as pltpu
from jax.sharding import PartitionSpec as P

F32, BF16 = jnp.float32, jnp.bfloat16
MESH = pl.DeviceIdType.MESH
GRID, NARROW, SECTION = 48, 4, 4
HIGH, RING, CORES = 2, 8, 2
WIDE = HIGH * RING * CORES
PLANES = GRID // NARROW
AREA = GRID * GRID
VECTORS = 12288
ROWS, COLS = VECTORS // 16, VECTORS // 32


def split_np(a):
    a = np.asarray(a, np.float32)
    h = a.astype(BF16)
    return h, (a - h.astype(np.float32)).astype(BF16)


def tables():
    k, x = np.arange(GRID)[:, None], np.arange(GRID)[None, :]
    c = math.sqrt(2.0 / GRID) * np.cos(math.pi * (2 * x + 1) * k / (2 * GRID))
    c[0] *= math.sqrt(0.5)
    cx = np.zeros((64, GRID))
    order = [p * PLANES + q for p in range(4) for q in range(8)] + [p * PLANES + q for p in range(4) for q in range(8, 12)]
    for i in range(GRID):
        cx[(i // 6) * 8 + i % 6] = c[i, order]
    h, l = split_np(cx)
    cx3 = np.concatenate([h, l, h], axis=1)
    bh, bl = split_np(np.kron(np.eye(16), c.T))
    h, l = split_np(c)
    cy3 = np.concatenate([h, l, h], axis=1)
    return cx3, bh, bl, cy3


def hi_lo(a):
    h = a.astype(BF16)
    return h, (a - h.astype(F32)).astype(BF16)


def dot(a, b):
    return lax.dot_general(a, b, (((1,), (0,)), ((), ())), preferred_element_type=F32)


def exchange_body(
    bands_ref, valence_ref, conduction_ref, out8_ref, out4_ref, stage8_ref, stage4_ref, send_sem, recv_sem
):
    me = lax.axis_index("narrow")
    barrier = pltpu.get_barrier_semaphore()
    for d in range(1, NARROW):
        pl.semaphore_signal(
            barrier, inc=1, device_id={"narrow": lax.rem(me + d, NARROW)}, device_id_type=MESH
        )
    for t in range(AREA // 128):
        conduction = conduction_ref[pl.ds(t, PLANES, stride=AREA // 128), :]
        lanes = slice(t * 128, (t + 1) * 128)
        for p in range(NARROW):
            valence = valence_ref[pl.ds(t * 8 + bands_ref[0, p], PLANES, stride=AREA // 16), :]
            density = valence * conduction
            stage8_ref[p, :, lanes] = density[:8]
            stage4_ref[p, :, lanes] = density[8:]
    out8_ref[me] = stage8_ref[me]
    out4_ref[me] = stage4_ref[me]
    pl.semaphore_wait(barrier, NARROW - 1)
    copies = []
    for d in range(1, NARROW):
        peer = lax.rem(me + d, NARROW)
        for part, (src, dst) in enumerate(((stage8_ref, out8_ref), (stage4_ref, out4_ref))):
            copy = pltpu.make_async_remote_copy(
                src_ref=src.at[peer],
                dst_ref=dst.at[me],
                send_sem=send_sem.at[part, d - 1],
                recv_sem=recv_sem.at[part, d - 1],
                device_id={"narrow": peer},
                device_id_type=MESH,
            )
            copy.start()
            copies.append(copy)
    for copy in copies:
        copy.wait()


def exchange(bands, valence, conduction):
    vmem = pl.BlockSpec(memory_space=pltpu.VMEM)
    return pl.pallas_call(
        exchange_body,
        out_shape=(
            jax.ShapeDtypeStruct((NARROW, 8, AREA), F32),
            jax.ShapeDtypeStruct((NARROW, 4, AREA), F32),
        ),
        in_specs=[pl.BlockSpec(memory_space=pltpu.SMEM), vmem, vmem],
        out_specs=(vmem, vmem),
        scratch_shapes=[
            pltpu.VMEM((NARROW, 8, AREA), F32),
            pltpu.VMEM((NARROW, 4, AREA), F32),
            pltpu.SemaphoreType.DMA((2, NARROW - 1)),
            pltpu.SemaphoreType.DMA((2, NARROW - 1)),
        ],
        compiler_params=pltpu.CompilerParams(
            collective_id=0, has_side_effects=True, vmem_limit_bytes=16 * 1024 * 1024
        ),
        cost_estimate=pl.CostEstimate(flops=10**10, bytes_accessed=2 * 10**7, transcendentals=0),
        name="exchange",
    )(bands, valence, conduction)


def polarize_body(
    bands_ref, ve_ref, ce_ref, freq_ref, d8_ref, d4_ref, gvec_ref, cx_ref, bh_ref, bl_ref, cy_ref,
    out_ref,
    rid_ref, lid_ref, z_ref, s_ref, t_ref, tt_ref, row_ref, col_ref, rows_ref, cols_ref, at_ref, bb_ref,
    send_small, send_row, send_side, send_col,
    recv_row1, recv_col1, recv_ring, recv_side, recv_y, recv_x, recv_xx,
):
    s, w, n = lax.axis_index("section"), lax.axis_index("wide"), lax.axis_index("narrow")
    yh, z, c = w // (RING * CORES), lax.rem(w // CORES, RING), lax.rem(w, CORES)
    me = s * NARROW + n

    def row_peer(d):
        sp, np_ = lax.rem(s + lax.rem(d, 4), SECTION), lax.rem(n + lax.rem(d // 4, 4), NARROW)
        wp = lax.rem(yh + d // 16, HIGH) * (RING * CORES) + z * CORES + c
        return sp, wp, np_

    def col_peer(d):
        return lax.rem(w + d, WIDE)

    barrier = pltpu.get_barrier_semaphore()

    def greet(d, carry):
        sp, wp, np_ = row_peer(d)
        pl.semaphore_signal(
            barrier, inc=1, device_id={"section": sp, "wide": wp, "narrow": np_}, device_id_type=MESH
        )
        pl.semaphore_signal(barrier, inc=1, device_id={"wide": col_peer(d)}, device_id_type=MESH)
        return carry

    lax.fori_loop(1, 32, greet, 0)

    gvec = gvec_ref[...]
    flat = gvec.astype(F32) + 0.5
    i = jnp.floor(flat * (1.0 / AREA)).astype(jnp.int32)
    ij = jnp.floor(flat * (1.0 / GRID)).astype(jnp.int32)
    group = jnp.floor((i.astype(F32) + 0.5) * (1.0 / 6)).astype(jnp.int32)
    lane = group * GRID + gvec - ij * GRID
    rid_ref[...] = ((i - group * 6) * 3 + (lane >> 7)) * GRID + ij - i * GRID
    lid_ref[...] = lane & 127

    valence = jnp.full((1, 256), ve_ref[bands_ref[0, n]], F32)
    conduction = jnp.full((1, 256), ce_ref[bands_ref[1, n]], F32)
    frequency = jnp.full((1, 256), freq_ref[0], F32)
    gap = conduction - valence
    weight = -4.0 * gap / (gap * gap + frequency * frequency) / math.sqrt(512.0)

    last = [jnp.concatenate([d4_ref[2 * q], d4_ref[2 * q + 1]], axis=0) for q in range(2)]
    dh, dl = hi_lo(jnp.concatenate([d8_ref[...].reshape(32, AREA), *last], axis=0))
    a = dot(cx_ref[...], jnp.concatenate([dh, dh, dl], axis=0))
    ah, al = hi_lo(a)
    third = AREA // 3
    lhs = jnp.concatenate(
        [half[:, b * third : (b + 1) * third] for half in (ah, al) for b in range(3)], axis=0
    )
    by_high = dot(lhs, bh_ref[...])
    by_low = dot(lhs[:192], bl_ref[...])
    for b in range(3):
        rows = slice(b * 64, (b + 1) * 64)
        z_ref[:, b * third : (b + 1) * third] = (
            by_high[rows] + by_high[192 + b * 64 : 256 + b * 64] + by_low[rows]
        )

    def relay(part, carry):
        lines = z_ref[:, pl.ds(pl.multiple_of(part * 384, 128), 384)]
        for y in range(8):
            s_ref[part * 8 + y] = jnp.concatenate(
                [lines[g * 8 : (g + 1) * 8, y * GRID : (y + 1) * GRID] for g in range(8)], axis=1
            )
        return carry

    lax.fori_loop(0, 6, relay, 0)
    for r in range(6):
        sh, sl = hi_lo(s_ref[:, r, :])
        t = dot(cy_ref[...], jnp.concatenate([sh, sh, sl], axis=0))
        for u in range(3):
            t_ref[(r * 3 + u) * GRID : (r * 3 + u + 1) * GRID, :] = t[:, u * 128 : (u + 1) * 128]
    th, tl = hi_lo(t_ref[...].T)
    tt_ref[0:128, :864] = th
    tt_ref[128:256, :864] = tl

    home = (z * CORES + c) * 32 + yh * 16 + me
    from_me = (z * CORES + c) * HIGH + yh

    def arrived(ref, sem):
        pltpu.make_async_copy(ref, ref, sem).wait()

    sends = []

    def send(src, dst, send_sem, recv_sem, **device):
        copy = pltpu.make_async_remote_copy(
            src_ref=src, dst_ref=dst, send_sem=send_sem, recv_sem=recv_sem, device_id=device, device_id_type=MESH
        )
        copy.start()
        sends.append(copy)

    for q in range(3):

        def chunk(k, carry, q=q):
            def pick(ref):
                return jnp.concatenate([ref[pl.ds(k * 6 + q, 1), :], ref[pl.ds(k * 6 + 3 + q, 1), :]], axis=1)

            rid, lid = pick(rid_ref), pick(lid_ref)
            acc = None
            for kt in range(4):
                kn = min(256, 864 - kt * 256)
                index = lax.broadcasted_iota(jnp.int32, (kn, 256), 0) + kt * 256
                hot = jnp.where(index == rid, 1.0, 0.0).astype(BF16)
                part = dot(tt_ref[:, kt * 256 : kt * 256 + kn], hot)
                acc = part if acc is None else acc + part
            both = acc[:128] + acc[128:]
            mine = lax.broadcasted_iota(jnp.int32, (128, 256), 0) == lid
            got = jnp.sum(jnp.where(mine, both, 0.0), axis=0, keepdims=True)
            heavy = got * weight
            row_ref[q * 16 + k, 0:1, :] = heavy[:, :128]
            row_ref[q * 16 + k, 1:2, :] = heavy[:, 128:]
            col_ref[q * 32 + 2 * k] = got[:, :128]
            col_ref[q * 32 + 2 * k + 1] = got[:, 128:]
            return carry

        lax.fori_loop(0, 16, chunk, 0)
        if q == 0:
            pl.semaphore_wait(barrier, 62)
        own_col = cols_ref.at[q * 512 + me * 32 + from_me]
        own_row = rows_ref.at[q * 512 + home]

        def spread(d, carry, q=q, own_row=own_row, own_col=own_col):
            sp, wp, np_ = row_peer(d)
            pltpu.make_async_remote_copy(
                src_ref=row_ref.at[q * 16 + sp * NARROW + np_], dst_ref=own_row, send_sem=send_small,
                recv_sem=recv_row1.at[q, d // 16],
                device_id={"section": sp, "wide": wp, "narrow": np_}, device_id_type=MESH,
            ).start()
            wc = col_peer(d)
            pltpu.make_async_remote_copy(
                src_ref=col_ref.at[q * 32 + wc], dst_ref=own_col, send_sem=send_small,
                recv_sem=recv_col1.at[q], device_id={"wide": wc}, device_id_type=MESH,
            ).start()
            return carry

        lax.fori_loop(1, 32, spread, 0)
        rows_ref[q * 512 + home] = row_ref[q * 16 + me]
        cols_ref[q * 512 + me * 32 + from_me] = col_ref[q * 32 + w]

    def sub(q, zz, cc, h):
        start = q * 512 + (zz * CORES + cc) * 32 + lax.rem(yh + h, HIGH) * 16
        return rows_ref.at[pl.ds(start, 16)]

    def ring_peer(step):
        return yh * (RING * CORES) + lax.rem(z + step + RING, RING) * CORES + c

    side = yh * (RING * CORES) + z * CORES + 1 - c

    def section_peer(step):
        return lax.rem(s + step + SECTION, SECTION)

    def cols_of(q, step, d):
        start = q * 512 + (section_peer(step) * NARROW + lax.rem(n - d + NARROW, NARROW)) * 32
        return cols_ref.at[pl.ds(start, 32)]

    ways = ((0, 1), (1, -1))

    def begin(q):
        mine = cols_of(q, 0, 0)
        arrived(cols_ref.at[pl.ds(q * 512, 31)], recv_col1.at[q])
        for d in range(1, NARROW):
            send(mine, mine, send_col, recv_y.at[q, d - 1], narrow=lax.rem(n + d, NARROW))
        for i, step in ways:
            send(mine, mine, send_col, recv_x.at[q, 0, i], section=section_peer(step))
        for h in range(2):
            arrived(rows_ref.at[pl.ds(q * 512, 15 + h)], recv_row1.at[q, h])
            block = sub(q, z, c, h)
            for i, step in ways:
                send(block, block, send_row, recv_ring.at[q, i, 0, h], wide=ring_peer(step))
            send(block, block, send_side, recv_side.at[q, 0, 0, h], wide=side)

    def ring_step(q, k):
        for h in range(2):
            for i, step in ways:
                if k == 4 and h != i:
                    continue
                got = sub(q, lax.rem(z - step * k + RING, RING), c, h)
                arrived(got, recv_ring.at[q, i, k - 1, h])
                if k < 3 or (k == 3 and h == i):
                    send(got, got, send_row, recv_ring.at[q, i, k, h], wide=ring_peer(step))
                send(got, got, send_side, recv_side.at[q, i, k, h], wide=side)

    def from_narrow(q, d):
        got = cols_of(q, 0, d)
        arrived(got, recv_y.at[q, d - 1])
        for i, step in ways:
            send(got, got, send_col, recv_x.at[q, d, i], section=section_peer(step))

    def along_section(q, d):
        i, step = ways[d % 2]
        got = cols_of(q, -step, d)
        arrived(got, recv_x.at[q, d, i])
        send(got, got, send_col, recv_xx.at[q, d], section=section_peer(step))

    def step(q, k):
        if k == 1:
            from_narrow(q, 1)
        elif k == 2:
            from_narrow(q, 3)
            from_narrow(q, 2)
            along_section(q, 0)
        elif k == 3:
            along_section(q, 1)
        ring_step(q, k)
        if k == 3:
            along_section(q, 3)
            along_section(q, 2)

    def finish(q):
        for d in range(NARROW):
            i, way = ways[1 - d % 2]
            arrived(cols_of(q, -way, d), recv_x.at[q, d, i])
            arrived(cols_of(q, 2, d), recv_xx.at[q, d])
        for h in range(2):
            arrived(sub(q, z, 1 - c, h), recv_side.at[q, 0, 0, h])
            for k in range(1, 5):
                for i, way in ways:
                    if k == 4 and h != i:
                        continue
                    arrived(sub(q, lax.rem(z - way * k + RING, RING), 1 - c, h), recv_side.at[q, i, k, h])
        lines = rows_ref.reshape(3072, 128)
        for half in range(2):
            left = lines[pl.ds(q * 1024 + half, 512, stride=2), :]
            lh, ll = hi_lo(left.T)
            here = slice(q * 256 + half * 128, q * 256 + half * 128 + 128)
            at_ref[here, 0:512] = lh
            at_ref[here, 512:1024] = lh
            at_ref[here, 1024:1536] = ll
        lines = cols_ref.reshape(1536, 128)
        right = jnp.concatenate(
            [lines[pl.ds(q * 512 + place, 16, stride=32), :] for place in range(32)], axis=0
        )
        rh, rl = hi_lo(right)
        here = slice(q * 128, q * 128 + 128)
        bb_ref[0:512, here] = rh
        bb_ref[512:1024, here] = rl
        bb_ref[1024:1536, here] = rh

    def multiply(q0, q1, c0, c1):
        part = dot(at_ref[q0 * 256 : q1 * 256, :], bb_ref[:, c0 * 128 : c1 * 128])
        for q in range(q0, q1):
            for half in range(2):
                first = (q - q0) * 256 + half * 128
                out_ref[half * 384 + q * 128 : half * 384 + q * 128 + 128, c0 * 128 : c1 * 128] = part[
                    first : first + 128
                ]

    begin(0)
    step(0, 1)
    begin(1)
    step(0, 2)
    step(1, 1)
    begin(2)
    step(0, 3)
    step(1, 2)
    step(2, 1)
    step(0, 4)
    step(1, 3)
    step(2, 2)
    step(1, 4)
    step(2, 3)
    finish(0)
    finish(1)
    multiply(0, 2, 0, 2)
    step(2, 4)
    finish(2)
    multiply(0, 2, 2, 3)
    multiply(2, 3, 0, 3)
    for copy in sends:
        copy.wait_send()
    for q in range(3):
        arrived(rows_ref.at[pl.ds(q * 512, 31)], send_small)
        arrived(cols_ref.at[pl.ds(q * 512, 31)], send_small)


def polarize(bands, ve, ce, freq, d8, d4, gvec):
    smem, vmem = pl.BlockSpec(memory_space=pltpu.SMEM), pl.BlockSpec(memory_space=pltpu.VMEM)
    dma = pltpu.SemaphoreType.DMA
    return pl.pallas_call(
        polarize_body,
        out_shape=jax.ShapeDtypeStruct((ROWS, COLS), F32),
        in_specs=[smem] * 4 + [vmem] * 7,
        out_specs=vmem,
        scratch_shapes=[
            pltpu.VMEM((96, 128), jnp.int32),
            pltpu.VMEM((96, 128), jnp.int32),
            pltpu.VMEM((64, AREA), F32),
            pltpu.VMEM((GRID, 8, 384), F32),
            pltpu.VMEM((864, 128), F32),
            pltpu.VMEM((256, 896), BF16),
            pltpu.VMEM((48, 2, 128), F32),
            pltpu.VMEM((96, 1, 128), F32),
            pltpu.VMEM((1536, 2, 128), F32),
            pltpu.VMEM((1536, 1, 128), F32),
            pltpu.VMEM((ROWS, 1536), BF16),
            pltpu.VMEM((1536, COLS), BF16),
            dma, dma, dma, dma,
            dma((3, 2)), dma((3,)), dma((3, 2, 4, 2)), dma((3, 2, 5, 2)), dma((3, 3)), dma((3, 4, 2)), dma((3, 4)),
        ],
        compiler_params=pltpu.CompilerParams(
            collective_id=1, has_side_effects=True, vmem_limit_bytes=40 * 1024 * 1024
        ),
        name="polarize",
    )(bands, ve, ce, freq, d8, d4, gvec, *[jnp.asarray(t) for t in tables()])


def on_device(ve_orb, ce_orb, ve, ce, freq, bands, gvec):
    tiles = AREA // 128
    valence = ve_orb.reshape(8, PLANES, tiles, 128).transpose(1, 2, 0, 3).reshape(-1, 128)
    conduction = ce_orb.reshape(PLANES * tiles, 128)
    d8, d4 = exchange(bands.T, valence, conduction)
    return polarize(bands.T, ve, ce, freq, d8, d4, gvec.reshape(96, 128))


def solution(mesh):
    in_specs = (
        P(None, "narrow", None),
        P(("section", "wide"), "narrow", None),
        P(),
        P(),
        P(),
        P(("section", "wide"), None),
        P(),
    )
    return jax.shard_map(
        on_device,
        mesh=mesh,
        in_specs=in_specs,
        out_specs=P(("section", "narrow"), "wide"),
        check_vma=False,
    )
```

time: 92.6 us -> 79.8 us (0.86)
  the two profiles are of different devices: /device:TPU:48 before, /device:TPU:1 now
where the time goes in v2:
time: 79.8 us; the launch traced here: 79.6 us
  Pallas kernels  75 us (94%)
  local copies, waits for them, and re-layouts  3.79 us (5%)
    pallas_call x1, Pallas kernels, polarize(): pl.pallas_call(polarize_body, out_shape=jax.ShapeDtypeStruct((ROWS, COLS)...  64.7 us
    pallas_call x1, Pallas kernels, exchange(): pl.pallas_call(exchange_body, out_shape=(jax.ShapeDtypeStruct((NARROW, 8,...  10.3 us
    unnamed x23, local copies, waits for them, and re-layouts  3.79 us

profile of v2, /device:TPU:1, one launch (start us, length us, event | category | flops | bytes accessed | tf_op | source)
XLA Modules:
  0.0 79.6 jit_solution(5939760994809257366)
XLA Ops:
  0.7 0.0 copy-start.5
  0.7 0.7 copy-done.5
  1.3 0.0 copy-start.9
  1.3 1.2 %copy-done.9 = f32[8,12,2304]{2,0,1:T(8,128)S(1)} copy-done((f32[8,12,2304]{2,0,1:T(8,128)S(1)}, f32[8,12,2304]{2,0,1:T(8,128)}, u32[]{:S(2)}) %copy-start.9) | copy-done | bytes 884760
  2.5 0.0 copy-start.10
  2.5 0.9 %copy-done.10 = f32[1,12,2304]{2,0,1:T(1,128)S(1)} copy-done((f32[1,12,2304]{2,0,1:T(1,128)S(1)}, f32[1,12,2304]{2,0,1:T(1,128)}, u32[]{:S(2)}) %copy-start.10) | copy-done | bytes 110616
  3.4 0.0 copy-start
  3.4 0.0 copy-start.1
  3.4 0.0 copy-start.2
  3.4 0.0 copy-start.3
  3.4 0.0 copy-start.4
  3.4 0.0 copy-start.6
  3.4 0.0 copy-start.7
  3.4 0.0 copy-start.8
  3.5 10.3 %exchange.1 = (f32[4,8,2304]{2,1,0:T(8,128)S(1)}, f32[4,4,2304]{2,1,0:T(4,128)S(1)}) custom-call(s32[2,4]{1,0:T(2,128)S(1)} %bitcast.9, f32[1728,128]{1,0:T(8,128)S(1)} %bitcast.11, f32[216,128]{1,0:T(8,128)S(1)} %bitcast.12), custom_call_target="tpu_custom_call" | custom-call | flops 10000000000 | bytes 20000000 | tf_op jit(solution)/shard_map/exchange/pallas_call | solution.py:94
  13.8 0.0 copy-done
  13.8 0.0 copy-done.1
  13.8 0.0 copy-done.2
  13.8 0.0 copy-done.3
  13.8 0.0 copy-done.4
  13.9 0.0 copy-done.6
  13.9 0.0 copy-done.7
  13.9 0.0 copy-done.8
  13.9 64.7 %polarize.1 = f32[768,384]{1,0:T(8,128)S(1)} custom-call(s32[2,4]{1,0:T(2,128)S(1)} %bitcast.10, f32[8]{0:T(128)S(1)} %copy-done.7, f32[128]{0:T(128)S(1)} %copy-done.8, f32[1]{0:T(128)S(6)} %copy.13.freq_ref, f32[4,8,2304]{2,1,0:T(8,128)S(1)} %get-tuple-element.7.d8_ref, f32[4,4,2304]{2,1,0:T(4,128)S(1)} %get-tuple-element.8.d4_ref, s32[96,128]{1,0:T(8,128)S(1)} %bitcast.8, ...), custom_call_target="tpu_custom_call" | custom-call | tf_op jit(solution)/shard_map/polarize/pallas_call | solution.py:398
  78.6 1.0 %copy.14 = f32[768,384]{1,0:T(8,128)} copy(f32[768,384]{1,0:T(8,128)S(1)} %polarize.1) | data formatting | bytes 2359296
Async XLA Ops:
  0.7 0.7 copy-start.5
  1.3 1.2 %copy-start.9 = (f32[8,12,2304]{2,0,1:T(8,128)S(1)}, f32[8,12,2304]{2,0,1:T(8,128)}, u32[]{:S(2)}) copy-start(f32[8,12,2304]{2,0,1:T(8,128)} %param.11) | copy-start | bytes 2654212
  2.5 0.9 %copy-start.10 = (f32[1,12,2304]{2,0,1:T(1,128)S(1)}, f32[1,12,2304]{2,0,1:T(1,128)}, u32[]{:S(2)}) copy-start(f32[1,12,2304]{2,0,1:T(1,128)} %param.12) | copy-start | bytes 331780
  3.4 10.4 %copy-start = (bf16[768,768]{1,0:T(8,128)(2,1)S(1)}, bf16[768,768]{1,0:T(8,128)(2,1)}, u32[]{:S(2)}) copy-start(bf16[768,768]{1,0:T(8,128)(2,1)} %constant.10.clone.bl_ref) | copy-start | bytes 3538948
  3.4 10.4 %copy-start.1 = (bf16[768,768]{1,0:T(8,128)(2,1)S(1)}, bf16[768,768]{1,0:T(8,128)(2,1)}, u32[]{:S(2)}) copy-start(bf16[768,768]{1,0:T(8,128)(2,1)} %constant.9.clone.bh_ref) | copy-start | bytes 3538948
  3.4 10.4 %copy-start.2 = (s32[12288]{0:T(1024)S(1)}, s32[12288]{0:T(1024)}, u32[]{:S(2)}) copy-start(s32[12288]{0:T(1024)} %param.17) | copy-start | bytes 147460
  3.4 10.4 %copy-start.3 = (bf16[64,144]{1,0:T(8,128)(2,1)S(1)}, bf16[64,144]{1,0:T(8,128)(2,1)}, u32[]{:S(2)}) copy-start(bf16[64,144]{1,0:T(8,128)(2,1)} %constant.8.clone.cx_ref) | copy-start | bytes 55300
  3.4 10.4 %copy-start.4 = (bf16[48,144]{1,0:T(8,128)(2,1)S(1)}, bf16[48,144]{1,0:T(8,128)(2,1)}, u32[]{:S(2)}) copy-start(bf16[48,144]{1,0:T(8,128)(2,1)} %constant.11.clone.cy_ref) | copy-start | bytes 41476
  3.4 10.4 %copy-start.6 = (s32[4,2]{0,1:T(2,128)S(1)}, s32[4,2]{0,1:T(2,128)}, u32[]{:S(2)}) copy-start(s32[4,2]{0,1:T(2,128)} %param.16) | copy-start | bytes 100
  3.4 10.4 %copy-start.7 = (f32[8]{0:T(128)S(1)}, f32[8]{0:T(128)}, u32[]{:S(2)}) copy-start(f32[8]{0:T(128)} %ve_ref.1) | copy-start | bytes 100
  3.4 10.4 %copy-start.8 = (f32[128]{0:T(128)S(1)}, f32[128]{0:T(128)}, u32[]{:S(2)}) copy-start(f32[128]{0:T(128)} %ce_ref.1) | copy-start | bytes 1540

commit v3 on v2

--- a/solution.py
+++ b/solution.py
@@ -36,7 +36,7 @@
         cx[(i // 6) * 8 + i % 6] = c[i, order]
     h, l = split_np(cx)
     cx3 = np.concatenate([h, l, h], axis=1)
-    bh, bl = split_np(np.kron(np.eye(16), c.T))
+    bh, bl = split_np(np.kron(np.eye(8), c.T))
     h, l = split_np(c)
     cy3 = np.concatenate([h, l, h], axis=1)
     return cx3, bh, bl, cy3
@@ -52,7 +52,9 @@
 
 
 def exchange_body(
-    bands_ref, valence_ref, conduction_ref, out8_ref, out4_ref, stage8_ref, stage4_ref, send_sem, recv_sem
+    bands_hbm, valence_hbm, conduction_hbm, bh_hbm, bl_hbm, cx_hbm,
+    s_ref,
+    bands_ref, valence_ref, conduction_ref, bh_ref, bl_ref, cx_ref, stage8_ref, stage4_ref, d8_ref, d4_ref, z_ref, load_sem, send_sem, recv_sem,
 ):
     me = lax.axis_index("narrow")
     barrier = pltpu.get_barrier_semaphore()
@@ -60,6 +62,23 @@
         pl.semaphore_signal(
             barrier, inc=1, device_id={"narrow": lax.rem(me + d, NARROW)}, device_id_type=MESH
         )
+    loads = [
+        pltpu.make_async_copy(src, dst, load_sem.at[i])
+        for i, (src, dst) in enumerate(
+            (
+                (bands_hbm, bands_ref),
+                (conduction_hbm, conduction_ref),
+                (valence_hbm, valence_ref),
+                (cx_hbm, cx_ref),
+                (bh_hbm, bh_ref),
+                (bl_hbm, bl_ref),
+            )
+        )
+    ]
+    for load in loads:
+        load.start()
+    for load in loads[:3]:
+        load.wait()
     for t in range(AREA // 128):
         conduction = conduction_ref[pl.ds(t, PLANES, stride=AREA // 128), :]
         lanes = slice(t * 128, (t + 1) * 128)
@@ -68,55 +87,93 @@
             density = valence * conduction
             stage8_ref[p, :, lanes] = density[:8]
             stage4_ref[p, :, lanes] = density[8:]
-    out8_ref[me] = stage8_ref[me]
-    out4_ref[me] = stage4_ref[me]
     pl.semaphore_wait(barrier, NARROW - 1)
+    third = AREA // 3
     copies = []
-    for d in range(1, NARROW):
-        peer = lax.rem(me + d, NARROW)
-        for part, (src, dst) in enumerate(((stage8_ref, out8_ref), (stage4_ref, out4_ref))):
-            copy = pltpu.make_async_remote_copy(
-                src_ref=src.at[peer],
-                dst_ref=dst.at[me],
-                send_sem=send_sem.at[part, d - 1],
-                recv_sem=recv_sem.at[part, d - 1],
-                device_id={"narrow": peer},
-                device_id_type=MESH,
-            )
-            copy.start()
-            copies.append(copy)
+    for b in range(3):
+        lanes = slice(b * third, (b + 1) * third)
+        for d in range(1, NARROW):
+            peer = lax.rem(me + d, NARROW)
+            for part, (src, dst) in enumerate(((stage8_ref, d8_ref), (stage4_ref, d4_ref))):
+                copy = pltpu.make_async_remote_copy(
+                    src_ref=src.at[peer, :, lanes],
+                    dst_ref=dst.at[me, :, lanes],
+                    send_sem=send_sem.at[b, part, d - 1],
+                    recv_sem=recv_sem.at[b, part, d - 1],
+                    device_id={"narrow": peer},
+                    device_id_type=MESH,
+                )
+                copy.start()
+                copies.append(copy)
+    d8_ref[me] = stage8_ref[me]
+    d4_ref[me] = stage4_ref[me]
+    for load in loads[3:]:
+        load.wait()
+    per_third = len(copies) // 3
+    for b in range(3):
+        for copy in copies[b * per_third : (b + 1) * per_third]:
+            copy.wait_recv()
+        lanes = slice(b * third, (b + 1) * third)
+        planes = [d8_ref[q, :, lanes] for q in range(NARROW)]
+        planes += [
+            jnp.concatenate([d4_ref[2 * q, :, lanes], d4_ref[2 * q + 1, :, lanes]], axis=0) for q in range(2)
+        ]
+        dh, dl = hi_lo(jnp.concatenate(planes, axis=0))
+        a = dot(cx_ref[...], jnp.concatenate([dh, dh, dl], axis=0))
+        ah, al = hi_lo(a)
+        lhs = jnp.concatenate([ah[:, :384], ah[:, 384:], al[:, :384], al[:, 384:]], axis=0)
+        by_high = dot(lhs, bh_ref[...])
+        by_low = dot(lhs[:128], bl_ref[...])
+        z_ref[...] = by_high[:128] + by_high[128:] + by_low
+
+        def relay(half, carry, b=b):
+            lines = z_ref[pl.ds(pl.multiple_of(half * 64, 64), 64), :]
+            for y in range(8):
+                s_ref[b * 16 + half * 8 + y] = jnp.concatenate(
+                    [lines[g * 8 : (g + 1) * 8, y * GRID : (y + 1) * GRID] for g in range(8)], axis=1
+                )
+            return carry
+
+        lax.fori_loop(0, 2, relay, 0)
     for copy in copies:
-        copy.wait()
-
-
-def exchange(bands, valence, conduction):
-    vmem = pl.BlockSpec(memory_space=pltpu.VMEM)
+        copy.wait_send()
+
+
+def exchange(bands, valence, conduction, cx3, bh, bl):
+    vmem, hbm = pl.BlockSpec(memory_space=pltpu.VMEM), pl.BlockSpec(memory_space=pltpu.HBM)
     return pl.pallas_call(
         exchange_body,
-        out_shape=(
-            jax.ShapeDtypeStruct((NARROW, 8, AREA), F32),
-            jax.ShapeDtypeStruct((NARROW, 4, AREA), F32),
-        ),
-        in_specs=[pl.BlockSpec(memory_space=pltpu.SMEM), vmem, vmem],
-        out_specs=(vmem, vmem),
+        out_shape=jax.ShapeDtypeStruct((GRID, 8, 384), F32),
+        in_specs=[hbm] * 6,
+        out_specs=vmem,
         scratch_shapes=[
+            pltpu.SMEM((2, NARROW), jnp.int32),
+            pltpu.VMEM(valence.shape, F32),
+            pltpu.VMEM(conduction.shape, F32),
+            pltpu.VMEM((384, 384), BF16),
+            pltpu.VMEM((384, 384), BF16),
+            pltpu.VMEM(cx3.shape, BF16),
             pltpu.VMEM((NARROW, 8, AREA), F32),
             pltpu.VMEM((NARROW, 4, AREA), F32),
-            pltpu.SemaphoreType.DMA((2, NARROW - 1)),
-            pltpu.SemaphoreType.DMA((2, NARROW - 1)),
+            pltpu.VMEM((NARROW, 8, AREA), F32),
+            pltpu.VMEM((NARROW, 4, AREA), F32),
+            pltpu.VMEM((128, 384), F32),
+            pltpu.SemaphoreType.DMA((6,)),
+            pltpu.SemaphoreType.DMA((3, 2, NARROW - 1)),
+            pltpu.SemaphoreType.DMA((3, 2, NARROW - 1)),
         ],
         compiler_params=pltpu.CompilerParams(
             collective_id=0, has_side_effects=True, vmem_limit_bytes=16 * 1024 * 1024
         ),
         cost_estimate=pl.CostEstimate(flops=10**10, bytes_accessed=2 * 10**7, transcendentals=0),
         name="exchange",
-    )(bands, valence, conduction)
+    )(*(pltpu.with_memory_space_constraint(a, pltpu.HBM) for a in (bands, valence, conduction, bh, bl, cx3)))
 
 
 def polarize_body(
-    bands_ref, ve_ref, ce_ref, freq_ref, d8_ref, d4_ref, gvec_ref, cx_ref, bh_ref, bl_ref, cy_ref,
+    bands_ref, ve_ref, ce_ref, freq_ref, s_ref, gvec_ref, cy_ref,
     out_ref,
-    rid_ref, lid_ref, z_ref, s_ref, t_ref, tt_ref, row_ref, col_ref, rows_ref, cols_ref, at_ref, bb_ref,
+    rid_ref, lid_ref, t_ref, tt_ref, row_ref, col_ref, rows_ref, cols_ref, at_ref, bb_ref,
     send_small, send_row, send_side, send_col,
     recv_row1, recv_col1, recv_ring, recv_side, recv_y, recv_x, recv_xx,
 ):
@@ -159,31 +216,6 @@
     gap = conduction - valence
     weight = -4.0 * gap / (gap * gap + frequency * frequency) / math.sqrt(512.0)
 
-    last = [jnp.concatenate([d4_ref[2 * q], d4_ref[2 * q + 1]], axis=0) for q in range(2)]
-    dh, dl = hi_lo(jnp.concatenate([d8_ref[...].reshape(32, AREA), *last], axis=0))
-    a = dot(cx_ref[...], jnp.concatenate([dh, dh, dl], axis=0))
-    ah, al = hi_lo(a)
-    third = AREA // 3
-    lhs = jnp.concatenate(
-        [half[:, b * third : (b + 1) * third] for half in (ah, al) for b in range(3)], axis=0
-    )
-    by_high = dot(lhs, bh_ref[...])
-    by_low = dot(lhs[:192], bl_ref[...])
-    for b in range(3):
-        rows = slice(b * 64, (b + 1) * 64)
-        z_ref[:, b * third : (b + 1) * third] = (
-            by_high[rows] + by_high[192 + b * 64 : 256 + b * 64] + by_low[rows]
-        )
-
-    def relay(part, carry):
-        lines = z_ref[:, pl.ds(pl.multiple_of(part * 384, 128), 384)]
-        for y in range(8):
-            s_ref[part * 8 + y] = jnp.concatenate(
-                [lines[g * 8 : (g + 1) * 8, y * GRID : (y + 1) * GRID] for g in range(8)], axis=1
-            )
-        return carry
-
-    lax.fori_loop(0, 6, relay, 0)
     for r in range(6):
         sh, sl = hi_lo(s_ref[:, r, :])
         t = dot(cy_ref[...], jnp.concatenate([sh, sh, sl], axis=0))
@@ -210,7 +242,7 @@
 
     for q in range(3):
 
-        def chunk(k, carry, q=q):
+        def chunk(k, q=q):
             def pick(ref):
                 return jnp.concatenate([ref[pl.ds(k * 6 + q, 1), :], ref[pl.ds(k * 6 + 3 + q, 1), :]], axis=1)
 
@@ -230,9 +262,13 @@
             row_ref[q * 16 + k, 1:2, :] = heavy[:, 128:]
             col_ref[q * 32 + 2 * k] = got[:, :128]
             col_ref[q * 32 + 2 * k + 1] = got[:, 128:]
+
+        def chunks(group, carry, chunk=chunk):
+            for k in range(8):
+                chunk(group * 8 + k)
             return carry
 
-        lax.fori_loop(0, 16, chunk, 0)
+        lax.fori_loop(0, 2, chunks, 0)
         if q == 0:
             pl.semaphore_wait(barrier, 62)
         own_col = cols_ref.at[q * 512 + me * 32 + from_me]
@@ -285,7 +321,12 @@
             arrived(rows_ref.at[pl.ds(q * 512, 15 + h)], recv_row1.at[q, h])
             block = sub(q, z, c, h)
             for i, step in ways:
-                send(block, block, send_row, recv_ring.at[q, i, 0, h], wide=ring_peer(step))
+                if q < 2:
+                    send(block, block, send_row, recv_ring.at[q, i, 0, h], wide=ring_peer(step))
+                    continue
+                for k in (4, 3, 2, 1):
+                    if k < 4 or h == i:
+                        send(block, block, send_row, recv_ring.at[q, i, k - 1, h], wide=ring_peer(step * k))
             send(block, block, send_side, recv_side.at[q, 0, 0, h], wide=side)
 
     def ring_step(q, k):
@@ -295,7 +336,7 @@
                     continue
                 got = sub(q, lax.rem(z - step * k + RING, RING), c, h)
                 arrived(got, recv_ring.at[q, i, k - 1, h])
-                if k < 3 or (k == 3 and h == i):
+                if q < 2 and (k < 3 or (k == 3 and h == i)):
                     send(got, got, send_row, recv_ring.at[q, i, k, h], wide=ring_peer(step))
                 send(got, got, send_side, recv_side.at[q, i, k, h], wide=side)
 
@@ -392,19 +433,17 @@
         arrived(cols_ref.at[pl.ds(q * 512, 31)], send_small)
 
 
-def polarize(bands, ve, ce, freq, d8, d4, gvec):
+def polarize(bands, ve, ce, freq, lines, gvec, cy3):
     smem, vmem = pl.BlockSpec(memory_space=pltpu.SMEM), pl.BlockSpec(memory_space=pltpu.VMEM)
     dma = pltpu.SemaphoreType.DMA
     return pl.pallas_call(
         polarize_body,
         out_shape=jax.ShapeDtypeStruct((ROWS, COLS), F32),
-        in_specs=[smem] * 4 + [vmem] * 7,
+        in_specs=[smem] * 4 + [vmem] * 3,
         out_specs=vmem,
         scratch_shapes=[
             pltpu.VMEM((96, 128), jnp.int32),
             pltpu.VMEM((96, 128), jnp.int32),
-            pltpu.VMEM((64, AREA), F32),
-            pltpu.VMEM((GRID, 8, 384), F32),
             pltpu.VMEM((864, 128), F32),
             pltpu.VMEM((256, 896), BF16),
             pltpu.VMEM((48, 2, 128), F32),
@@ -420,15 +459,16 @@
             collective_id=1, has_side_effects=True, vmem_limit_bytes=40 * 1024 * 1024
         ),
         name="polarize",
-    )(bands, ve, ce, freq, d8, d4, gvec, *[jnp.asarray(t) for t in tables()])
+    )(bands, ve, ce, freq, lines, gvec, cy3)
 
 
 def on_device(ve_orb, ce_orb, ve, ce, freq, bands, gvec):
     tiles = AREA // 128
     valence = ve_orb.reshape(8, PLANES, tiles, 128).transpose(1, 2, 0, 3).reshape(-1, 128)
     conduction = ce_orb.reshape(PLANES * tiles, 128)
-    d8, d4 = exchange(bands.T, valence, conduction)
-    return polarize(bands.T, ve, ce, freq, d8, d4, gvec.reshape(96, 128))
+    cx3, bh, bl, cy3 = (jnp.asarray(t) for t in tables())
+    lines = exchange(bands.T, valence, conduction, cx3, bh, bl)
+    return polarize(bands.T, ve, ce, freq, lines, gvec.reshape(96, 128), cy3)
 
 
 def solution(mesh):

time: 79.8 us -> 69.3 us (0.87)
  Pallas kernels: 75 us -> 67.3 us
  local copies, waits for them, and re-layouts: 3.79 us -> 1.04 us
    pallas_call x1, Pallas kernels: 64.7 us -> 55.4 us  [polarize(): pl.pallas_call(polarize_body, out_shape=jax.ShapeDtypeStruct((ROWS, COLS)...]
    unnamed x23 -> x11, local copies, waits for them, and re-layouts: 3.79 us -> 1.04 us
    pallas_call x1, Pallas kernels: 10.3 us -> 11.9 us  [exchange(): pl.pallas_call(exchange_body, out_shape=jax.ShapeDtypeStruct((GRID, 8, 38...]
where the time goes in v3:
time: 69.3 us; the launch traced here: 69.1 us
  Pallas kernels  67.3 us (97%)
  local copies, waits for them, and re-layouts  1.04 us (2%)
  between operations  0.75 us (1%)
    pallas_call x1, Pallas kernels, polarize(): pl.pallas_call(polarize_body, out_shape=jax.ShapeDtypeStruct((ROWS, COLS)...  55.4 us
    pallas_call x1, Pallas kernels, exchange(): pl.pallas_call(exchange_body, out_shape=jax.ShapeDtypeStruct((GRID, 8, 38...  11.9 us

profile of v3, /device:TPU:1, one launch (start us, length us, event | category | flops | bytes accessed | tf_op | source)
XLA Modules:
  0.0 69.1 jit_solution(13810992377531694069)
XLA Ops:
  0.7 0.0 copy-start
  0.7 0.0 copy-start.1
  0.7 0.0 copy-start.2
  0.7 0.0 copy-start.3
  0.7 0.0 copy-start.4
  0.7 11.9 %exchange.1.s_ref = f32[48,8,384]{2,1,0:T(8,128)S(1)} custom-call(s32[2,4]{1,0:T(2,128)} %bitcast.9, f32[1728,128]{1,0:T(8,128)} %bitcast.11, f32[216,128]{1,0:T(8,128)} %bitcast.12, bf16[384,384]{1,0:T(8,128)(2,1)} %constant.9.clone.bh_hbm, bf16[384,384]{1,0:T(8,128)(2,1)} %constant.10.clone.bl_hbm, bf16[64,144]{1,0:T(8,128)(2,1)} %constant.8.clone.cx_hbm), custom_call_target="tpu_custom_call" | custom-call | flops 10000000000 | bytes 20000000 | tf_op jit(solution)/shard_map/exchange/pallas_call | solution.py:144
  12.6 0.0 copy-done
  12.6 0.0 copy-done.1
  12.6 0.0 copy-done.2
  12.6 0.0 copy-done.3
  12.7 0.0 copy-done.4
  12.7 55.4 %polarize.1 = f32[768,384]{1,0:T(8,128)S(1)} custom-call(s32[2,4]{1,0:T(2,128)S(1)} %bitcast.10, f32[8]{0:T(128)S(1)} %copy-done.3, f32[128]{0:T(128)S(1)} %copy-done.4, f32[1]{0:T(128)S(6)} %copy.13.freq_ref, f32[48,8,384]{2,1,0:T(8,128)S(1)} %exchange.1.s_ref, s32[96,128]{1,0:T(8,128)S(1)} %bitcast.8, bf16[48,144]{1,0:T(8,128)(2,1)S(1)} %copy-done.1), custom_call_target="tpu_custom_call" | custom-call | tf_op jit(solution)/shard_map/polarize/pallas_call | solution.py:439
  68.0 1.0 %copy.14 = f32[768,384]{1,0:T(8,128)} copy(f32[768,384]{1,0:T(8,128)S(1)} %polarize.1) | data formatting | bytes 2359296
Async XLA Ops:
  0.7 12.0 %copy-start = (s32[12288]{0:T(1024)S(1)}, s32[12288]{0:T(1024)}, u32[]{:S(2)}) copy-start(s32[12288]{0:T(1024)} %param.17) | copy-start | bytes 147460
  0.7 12.0 %copy-start.1 = (bf16[48,144]{1,0:T(8,128)(2,1)S(1)}, bf16[48,144]{1,0:T(8,128)(2,1)}, u32[]{:S(2)}) copy-start(bf16[48,144]{1,0:T(8,128)(2,1)} %constant.11.clone.cy_ref) | copy-start | bytes 41476
  0.7 12.0 %copy-start.2 = (s32[4,2]{0,1:T(2,128)S(1)}, s32[4,2]{0,1:T(2,128)}, u32[]{:S(2)}) copy-start(s32[4,2]{0,1:T(2,128)} %param.16) | copy-start | bytes 100
  0.7 12.0 %copy-start.3 = (f32[8]{0:T(128)S(1)}, f32[8]{0:T(128)}, u32[]{:S(2)}) copy-start(f32[8]{0:T(128)} %ve_ref.1) | copy-start | bytes 100
  0.7 12.0 %copy-start.4 = (f32[128]{0:T(128)S(1)}, f32[128]{0:T(128)}, u32[]{:S(2)}) copy-start(f32[128]{0:T(128)} %ce_ref.1) | copy-start | bytes 1540

commit v4 on v3

--- a/solution.py
+++ b/solution.py
@@ -310,21 +310,23 @@
 
     ways = ((0, 1), (1, -1))
 
+    def to_section(q, d, block):
+        for i, step in ways:
+            send(block, block, send_col, recv_x.at[q, d, i], section=section_peer(step))
+        if q == 2:
+            send(block, block, send_col, recv_xx.at[q, d], section=section_peer(2))
+
     def begin(q):
         mine = cols_of(q, 0, 0)
         arrived(cols_ref.at[pl.ds(q * 512, 31)], recv_col1.at[q])
         for d in range(1, NARROW):
             send(mine, mine, send_col, recv_y.at[q, d - 1], narrow=lax.rem(n + d, NARROW))
-        for i, step in ways:
-            send(mine, mine, send_col, recv_x.at[q, 0, i], section=section_peer(step))
+        to_section(q, 0, mine)
         for h in range(2):
             arrived(rows_ref.at[pl.ds(q * 512, 15 + h)], recv_row1.at[q, h])
             block = sub(q, z, c, h)
             for i, step in ways:
-                if q < 2:
-                    send(block, block, send_row, recv_ring.at[q, i, 0, h], wide=ring_peer(step))
-                    continue
-                for k in (4, 3, 2, 1):
+                for k in ((1,), (2, 1), (4, 3, 2, 1))[q]:
                     if k < 4 or h == i:
                         send(block, block, send_row, recv_ring.at[q, i, k - 1, h], wide=ring_peer(step * k))
             send(block, block, send_side, recv_side.at[q, 0, 0, h], wide=side)
@@ -336,15 +338,18 @@
                     continue
                 got = sub(q, lax.rem(z - step * k + RING, RING), c, h)
                 arrived(got, recv_ring.at[q, i, k - 1, h])
-                if q < 2 and (k < 3 or (k == 3 and h == i)):
+                if q == 0 and (k < 3 or (k == 3 and h == i)):
                     send(got, got, send_row, recv_ring.at[q, i, k, h], wide=ring_peer(step))
+                if q == 1 and k == 2:
+                    if h == i:
+                        send(got, got, send_row, recv_ring.at[q, i, 3, h], wide=ring_peer(2 * step))
+                    send(got, got, send_row, recv_ring.at[q, i, 2, h], wide=ring_peer(step))
                 send(got, got, send_side, recv_side.at[q, i, k, h], wide=side)
 
     def from_narrow(q, d):
         got = cols_of(q, 0, d)
         arrived(got, recv_y.at[q, d - 1])
-        for i, step in ways:
-            send(got, got, send_col, recv_x.at[q, d, i], section=section_peer(step))
+        to_section(q, d, got)
 
     def along_section(q, d):
         i, step = ways[d % 2]
@@ -368,8 +373,9 @@
 
     def finish(q):
         for d in range(NARROW):
-            i, way = ways[1 - d % 2]
-            arrived(cols_of(q, -way, d), recv_x.at[q, d, i])
+            for i, way in ways:
+                if q == 2 or i != d % 2:
+                    arrived(cols_of(q, -way, d), recv_x.at[q, d, i])
             arrived(cols_of(q, 2, d), recv_xx.at[q, d])
         for h in range(2):
             arrived(sub(q, z, 1 - c, h), recv_side.at[q, 0, 0, h])
@@ -413,16 +419,16 @@
     begin(2)
     step(0, 3)
     step(1, 2)
-    step(2, 1)
+    for d in (1, 3, 2):
+        from_narrow(2, d)
     step(0, 4)
     step(1, 3)
-    step(2, 2)
+    finish(0)
     step(1, 4)
-    step(2, 3)
-    finish(0)
+    for k in range(1, 5):
+        ring_step(2, k)
     finish(1)
     multiply(0, 2, 0, 2)
-    step(2, 4)
     finish(2)
     multiply(0, 2, 2, 3)
     multiply(2, 3, 0, 3)

time: 69.3 us -> 65.7 us (0.948)
  Pallas kernels: 67.3 us -> 63.7 us
    pallas_call x1, Pallas kernels: 55.4 us -> 51.8 us  [polarize(): pl.pallas_call(polarize_body, out_shape=jax.ShapeDtypeStruct((ROWS, COLS)...]
where the time goes in v4:
time: 65.7 us; the launch traced here: 65.5 us
  Pallas kernels  63.7 us (97%)
  local copies, waits for them, and re-layouts  1.04 us (2%)
  between operations  0.75 us (1%)
    pallas_call x1, Pallas kernels, polarize(): pl.pallas_call(polarize_body, out_shape=jax.ShapeDtypeStruct((ROWS, COLS)...  51.8 us
    pallas_call x1, Pallas kernels, exchange(): pl.pallas_call(exchange_body, out_shape=jax.ShapeDtypeStruct((GRID, 8, 38...  11.9 us

profile of v4, /device:TPU:1, one launch (start us, length us, event | category | flops | bytes accessed | tf_op | source)
XLA Modules:
  0.0 65.5 jit_solution(6028915164556136434)
XLA Ops:
  0.7 0.0 copy-start
  0.7 0.0 copy-start.1
  0.7 0.0 copy-start.2
  0.7 0.0 copy-start.3
  0.7 0.0 copy-start.4
  0.7 11.9 %exchange.1.s_ref = f32[48,8,384]{2,1,0:T(8,128)S(1)} custom-call(s32[2,4]{1,0:T(2,128)} %bitcast.9, f32[1728,128]{1,0:T(8,128)} %bitcast.11, f32[216,128]{1,0:T(8,128)} %bitcast.12, bf16[384,384]{1,0:T(8,128)(2,1)} %constant.9.clone.bh_hbm, bf16[384,384]{1,0:T(8,128)(2,1)} %constant.10.clone.bl_hbm, bf16[64,144]{1,0:T(8,128)(2,1)} %constant.8.clone.cx_hbm), custom_call_target="tpu_custom_call" | custom-call | flops 10000000000 | bytes 20000000 | tf_op jit(solution)/shard_map/exchange/pallas_call | solution.py:144
  12.6 0.0 copy-done
  12.6 0.0 copy-done.1
  12.6 0.0 copy-done.2
  12.6 0.0 copy-done.3
  12.6 0.0 copy-done.4
  12.7 51.8 %polarize.1 = f32[768,384]{1,0:T(8,128)S(1)} custom-call(s32[2,4]{1,0:T(2,128)S(1)} %bitcast.10, f32[8]{0:T(128)S(1)} %copy-done.3, f32[128]{0:T(128)S(1)} %copy-done.4, f32[1]{0:T(128)S(6)} %copy.13.freq_ref, f32[48,8,384]{2,1,0:T(8,128)S(1)} %exchange.1.s_ref, s32[96,128]{1,0:T(8,128)S(1)} %bitcast.8, bf16[48,144]{1,0:T(8,128)(2,1)S(1)} %copy-done.1), custom_call_target="tpu_custom_call" | custom-call | tf_op jit(solution)/shard_map/polarize/pallas_call | solution.py:445
  64.5 1.0 %copy.14 = f32[768,384]{1,0:T(8,128)} copy(f32[768,384]{1,0:T(8,128)S(1)} %polarize.1) | data formatting | bytes 2359296
Async XLA Ops:
  0.7 12.0 %copy-start = (s32[12288]{0:T(1024)S(1)}, s32[12288]{0:T(1024)}, u32[]{:S(2)}) copy-start(s32[12288]{0:T(1024)} %param.17) | copy-start | bytes 147460
  0.7 12.0 %copy-start.1 = (bf16[48,144]{1,0:T(8,128)(2,1)S(1)}, bf16[48,144]{1,0:T(8,128)(2,1)}, u32[]{:S(2)}) copy-start(bf16[48,144]{1,0:T(8,128)(2,1)} %constant.11.clone.cy_ref) | copy-start | bytes 41476
  0.7 12.0 %copy-start.2 = (s32[4,2]{0,1:T(2,128)S(1)}, s32[4,2]{0,1:T(2,128)}, u32[]{:S(2)}) copy-start(s32[4,2]{0,1:T(2,128)} %param.16) | copy-start | bytes 100
  0.7 12.0 %copy-start.3 = (f32[8]{0:T(128)S(1)}, f32[8]{0:T(128)}, u32[]{:S(2)}) copy-start(f32[8]{0:T(128)} %ve_ref.1) | copy-start | bytes 100
  0.7 12.0 %copy-start.4 = (f32[128]{0:T(128)S(1)}, f32[128]{0:T(128)}, u32[]{:S(2)}) copy-start(f32[128]{0:T(128)} %ce_ref.1) | copy-start | bytes 1540
